TPU v7x, 128 devices: a whole 4x4x4 slice. The times are simulated.
128 devices in a mesh: row: 8 (over y, core), col: 16 (over z, x).
Axes of the slice: x: 4, y: 4, z: 4, core: 2. Of those that a mesh axis runs over, the one named last changes fastest.
Arguments:
- coefficients: float32 [20480, 1024], P(('row', 'col')), may hold values from -24 to 24, as said below
Outputs:
- orbitals: float32 [20480, 1024], P(('row', 'col'))
Inputs may be any that keep to these rules, and one draw needn't show every extreme that they name: Real coefficients of full column rank.
All inputs are finite; a program needn't handle non-finite values.
Results may differ from a plain program's by a relative error of at most 0.00014.
Values sent between devices are 32-bit elements; how exact they have to be, the bound alone decides.
A program may use at most 64 MiB of HBM per device.

v0:
```python
import jax
import jax.numpy as jnp
from jax import lax

NG = 20480


def reference(coefficients):
    margin = (
        jnp.dot(
            coefficients.T,
            coefficients,
            precision=lax.Precision.HIGHEST,
            preferred_element_type=jnp.float32,
        )
        / NG
    )
    factor = jnp.linalg.cholesky(margin)
    solved = jax.scipy.linalg.solve_triangular(factor, coefficients.T, lower=True)
    return solved.T


def solution(mesh):
    return reference
```

profile of v0, /device:TPU:0, one launch (start us, length us, event | category | flops | bytes accessed | tf_op | source)
XLA Modules:
  0.0 516.8 jit_solution(2790187280139700041)
XLA Ops:
  6.5 6.8 %fusion.62 = f32[1024,1024]{0,1:T(8,128)} fusion(f32[160,1024]{1,0:T(8,128)} %param), kind=kOutput, calls=%fused_computation.156 | convolution fusion | flops 2013265920 | bytes 4849664 | tf_op jit(solution)/dot_general | solution.py:10
  13.4 157.0 %all-reduce.3.cloned.1.call-done = f32[1024,1024]{0,1:T(8,128)} async-done(((f32[1024,1024]{0,1:T(8,128)}), f32[1024,1024]{0,1:T(8,128)}) %all-reduce.3.cloned.1.call-update) | async-done | bytes 4194320 | tf_op jit(solution)/dot_general | solution.py:10
  170.4 5.1 broadcast_multiply_fusion
  175.5 5.6 %copy.3 = f32[1024,1024]{1,0:T(8,128)} copy(f32[1024,1024]{0,1:T(8,128)} %broadcast_multiply_fusion) | data formatting | bytes 8388608 | tf_op jit(solution)/div | solution.py:10
  181.1 4.5 fusion
  187.5 11.7 %cholesky.5 = f32[128,128]{1,0:T(8,128)S(1)} custom-call(f32[128,128]{1,0:T(8,128)S(1)} %cholesky.186), custom_call_target="Cholesky" | custom-call | tf_op jit(solution)/jit(cholesky)/cholesky | solution.py:18
  199.3 9.8 %custom-call.71 = f32[1,128,128]{1,2,0:T(8,128)S(1)} custom-call(f32[1,128,128]{2,1,0:T(8,128)S(1)} %get-tuple-element.68), custom_call_target="InvertDiagBlocksLowerTriangular" | custom-call | tf_op jit(solution)/jit(cholesky)/cholesky | solution.py:18
  209.1 2.5 cholesky.31
  211.6 2.4 constant_dynamic-update-slice_fusion.32
  215.5 12.2 %cholesky.23 = f32[128,128]{1,0:T(8,128)S(1)} custom-call(f32[128,128]{1,0:T(8,128)S(1)} %cholesky.192), custom_call_target="Cholesky" | custom-call | tf_op jit(solution)/jit(cholesky)/cholesky | solution.py:18
  228.4 9.8 %custom-call.72 = f32[1,128,128]{1,2,0:T(8,128)S(1)} custom-call(f32[1,128,128]{2,1,0:T(8,128)S(1)} %get-tuple-element.65), custom_call_target="InvertDiagBlocksLowerTriangular" | custom-call | tf_op jit(solution)/jit(cholesky)/cholesky | solution.py:18
  241.5 11.7 %cholesky.48 = f32[128,128]{1,0:T(8,128)S(1)} custom-call(f32[128,128]{1,0:T(8,128)S(1)} %cholesky.199), custom_call_target="Cholesky" | custom-call | tf_op jit(solution)/jit(cholesky)/cholesky | solution.py:18
  254.5 9.8 %custom-call.73 = f32[1,128,128]{1,2,0:T(8,128)S(1)} custom-call(f32[1,128,128]{2,1,0:T(8,128)S(1)} %get-tuple-element.62), custom_call_target="InvertDiagBlocksLowerTriangular" | custom-call | tf_op jit(solution)/jit(cholesky)/cholesky | solution.py:18
  265.5 2.3 convolution_subtract_fusion.2
  267.8 11.9 %cholesky.71 = f32[128,128]{1,0:T(8,128)S(1)} custom-call(f32[128,128]{1,0:T(8,128)S(1)} %cholesky.204), custom_call_target="Cholesky" | custom-call | tf_op jit(solution)/jit(cholesky)/cholesky | solution.py:18
  281.0 9.8 %custom-call.74 = f32[1,128,128]{1,2,0:T(8,128)S(1)} custom-call(f32[1,128,128]{2,1,0:T(8,128)S(1)} %get-tuple-element.59), custom_call_target="InvertDiagBlocksLowerTriangular" | custom-call | tf_op jit(solution)/jit(cholesky)/cholesky | solution.py:18
  291.9 2.3 convolution_subtract_fusion.3
  294.2 11.7 %cholesky.96 = f32[128,128]{1,0:T(8,128)S(1)} custom-call(f32[128,128]{1,0:T(8,128)S(1)} %cholesky.209), custom_call_target="Cholesky" | custom-call | tf_op jit(solution)/jit(cholesky)/cholesky | solution.py:18
  307.2 10.0 %custom-call.75 = f32[1,128,128]{1,2,0:T(8,128)S(1)} custom-call(f32[1,128,128]{2,1,0:T(8,128)S(1)} %get-tuple-element.56), custom_call_target="InvertDiagBlocksLowerTriangular" | custom-call | tf_op jit(solution)/jit(cholesky)/cholesky | solution.py:18
  318.3 2.3 convolution_subtract_fusion.4
  320.6 11.7 %cholesky.122 = f32[128,128]{1,0:T(8,128)S(1)} custom-call(f32[128,128]{1,0:T(8,128)S(1)} %cholesky.214), custom_call_target="Cholesky" | custom-call | tf_op jit(solution)/jit(cholesky)/cholesky | solution.py:18
  333.6 9.8 %custom-call.76 = f32[1,128,128]{1,2,0:T(8,128)S(1)} custom-call(f32[1,128,128]{2,1,0:T(8,128)S(1)} %get-tuple-element.53), custom_call_target="InvertDiagBlocksLowerTriangular" | custom-call | tf_op jit(solution)/jit(cholesky)/cholesky | solution.py:18
  346.4 12.1 %cholesky.148 = f32[128,128]{1,0:T(8,128)S(1)} custom-call(f32[128,128]{1,0:T(8,128)S(1)} %cholesky.221), custom_call_target="Cholesky" | custom-call | tf_op jit(solution)/jit(cholesky)/cholesky | solution.py:18
  359.7 9.8 %custom-call.77 = f32[1,128,128]{1,2,0:T(8,128)S(1)} custom-call(f32[1,128,128]{2,1,0:T(8,128)S(1)} %get-tuple-element.50), custom_call_target="InvertDiagBlocksLowerTriangular" | custom-call | tf_op jit(solution)/jit(cholesky)/cholesky | solution.py:18
  372.2 11.7 %cholesky.172 = f32[128,128]{1,0:T(8,128)S(1)} custom-call(f32[128,128]{1,0:T(8,128)S(1)} %convolution_subtract_fusion.13), custom_call_target="Cholesky" | custom-call | tf_op jit(solution)/jit(cholesky)/cholesky | solution.py:18
  390.7 4.9 select_select_fusion
  395.6 22.8 %while.1 = (s32[]{:T(128)}, f32[1024,1024]{1,0:T(8,128)}, s32[8,2]{0,1:T(2,128)S(1)}, f32[8,128,128]{2,1,0:T(8,128)S(1)}, s32[]{:T(128)}) while((s32[]{:T(128)}, f32[1024,1024]{1,0:T(8,128)}, s32[8,2]{0,1:T(2,128)S(1)}, f32[8,128,128]{2,1,0:T(8,128)S(1)}, s32[]{:T(128)}) %tuple.56), condition=%wide.while_cond, body=%wide.while_body.sunk | while | flops 2 | bytes 131181 | solution.py:19
  396.2 2.2 bitcast_dynamic-update-slice_fusion.2
  399.1 2.2 bitcast_dynamic-update-slice_fusion.2
  401.9 2.2 bitcast_dynamic-update-slice_fusion.2
  404.8 2.2 bitcast_dynamic-update-slice_fusion.2
  418.4 78.8 %custom-call.78 = f32[8,128,128]{1,2,0:T(8,128)S(1)} custom-call(f32[8,128,128]{2,1,0:T(8,128)S(1)} %get-tuple-element.11), custom_call_target="InvertDiagBlocksLowerTriangular" | custom-call | tf_op jit(solution)/jit(_solve_triangular)/triangular_solve | solution.py:19
  (78 shorter events, 51.1 us)
Async XLA Ops:
  6.5 163.9 %all-reduce.3.cloned.1.call-start = ((), (), s32[]{:S(2)}) async-start(), calls=%async_computation | async-start | bytes 8388608 | tf_op jit(solution)/dot_general | solution.py:10
  185.6 1.9 copy-start
  390.7 106.5 %copy-start.1 = (f32[160,1024]{1,0:T(8,128)S(1)}, f32[160,1024]{1,0:T(8,128)}, u32[]{:S(2)}) copy-start(f32[160,1024]{1,0:T(8,128)} %param) | copy-start | bytes 1966084
  508.9 0.8 copy-start.2
Sparse Core Ops, SparseCore 0:
  13.5 156.8 all-reduce.2
where the time goes:
time: 522 us; the launch traced here: 517 us
  other arithmetic  266 us (51%)
  waiting for transfers between devices  157 us (30%)
  matrix products  41.5 us (8%)
  local copies, waits for them, and re-layouts  33.6 us (6%)
  between operations  18.7 us (4%)
    another operation x30, other arithmetic, reference(): factor = jnp.linalg.cholesky(margin)  173 us
    dot_general x1, waiting for transfers between devices, reference(): jnp.dot(coefficients.T, coefficients, precision=lax.Precision.HIGHEST, pr...  157 us
    another operation x3, other arithmetic, reference(): jax.scipy.linalg.solve_triangular(factor, coefficients.T, lower=True)  83.6 us
    another operation x14, matrix products, reference(): factor = jnp.linalg.cholesky(margin)  23.1 us
    another operation x24, local copies, waits for them, and re-layouts  22.7 us
    another operation x15, matrix products, reference(): jax.scipy.linalg.solve_triangular(factor, coefficients.T, lower=True)  11.6 us
  transfers between devices with their start and end apart: 1, of which 1 were waited for; matrix products, arithmetic and copies ran while one was open for 0% of the time, Pallas kernels for 0%

commit v1 on v0

v1 whole, which is shorter than its diff:
```python
import jax
import jax.numpy as jnp
from jax import lax
from jax.experimental import pallas as pl
from jax.experimental.pallas import tpu as pltpu
from jax.sharding import PartitionSpec as P_

def bl(x, c):
    return jnp.broadcast_to(x[:, c:c+1], (8,128))
def bs(x, k):
    return jnp.broadcast_to(x[k:k+1, :], (8,128))

def leaf(W, nb=16):
    sub = lax.broadcasted_iota(jnp.int32, (8,128), 0)
    lane = lax.broadcasted_iota(jnp.int32, (8,128), 1)
    X = [jnp.where(lane == sub + 8*g, 1.0, 0.0).astype(jnp.float32) for g in range(nb)]
    W = list(W)
    out = []
    for g in range(nb):
        C = [[bl(W[h], 8*g+k) for k in range(8)] for h in range(g, nb)]
        fin = None
        for k in range(8):
            d = bs(C[0][k], k)
            r = lax.rsqrt(d)
            for c in C: c[k] = c[k]*r
            for j in range(k+1, 8):
                s = bs(C[0][k], j)
                for c in C: c[j] = c[j] - c[k]*s
            uW = bs(W[g], k)*r
            uX = bs(X[g], k)*r
            fin = uX if fin is None else jnp.where(sub == k, uX, fin)
            for i, c in enumerate(C):
                h = g+i
                if h == g and k == 7: continue
                W[h] = W[h] - c[k]*uW
                X[h] = X[h] - c[k]*uX
        out.append(fin)
    return out

NB=1024; R=160; LB=128; T=NB+R
F=jnp.float32; BF=jnp.bfloat16
NT=(((1,),(1,)),((),()))
def dnt(a,b): return lax.dot_general(a,b,NT,preferred_element_type=F)
def split(x):
    hi=x.astype(BF); lo=(x-hi.astype(F)).astype(BF)
    return hi,lo

def kern(g_ref, a_ref, q_ref, hi_ref, lo_ref, c_ref, xs_ref, d_ref, w_ref):
    hi_ref[...]=jnp.zeros_like(hi_ref); lo_ref[...]=jnp.zeros_like(lo_ref)
    c_ref[...]=jnp.zeros_like(c_ref); xs_ref[...]=jnp.zeros_like(xs_ref)
    def blk(p):
        return jnp.concatenate([g_ref[0,pl.ds(p*64,64),:],g_ref[1,pl.ds(p*64,64),:]],axis=0)
    d_ref[...]=blk(0)
    def splitx(x):
        xh,xl=split(x)
        return jnp.concatenate([xh,xl],axis=0)
    def mul3(ph,plo,r):
        t=dnt(ph,r)
        return t[:,:LB]+t[:,LB:]+dnt(plo,r[:LB])
    def body(kk,_):
        c0=pl.multiple_of(kk*LB,LB)
        off=kk*8-lax.shift_right_logical(kk*(kk-1),1)
        W=[d_ref[8*g:8*g+8,:] for g in range(16)]
        X=leaf(W)
        cp=pl.multiple_of(jnp.maximum(kk-1,0)*LB,LB)
        xs=xs_ref[...]
        for r0 in list(range(0,NB,LB))+[NB]:
            r1=min(r0+LB,T) if r0<NB else T
            ph,plo=split(c_ref[r0:r1,:])
            l=mul3(ph,plo,xs)
            h,lw=split(l)
            hi_ref[r0:r1,pl.ds(cp,LB)]=h; lo_ref[r0:r1,pl.ds(cp,LB)]=lw
            if r0==NB: q_ref[:,pl.ds(cp,LB)]=l
        rh=jnp.concatenate([hi_ref[pl.ds(c0,LB),:],lo_ref[pl.ds(c0,LB),:]],axis=0)
        for r0 in list(range(0,NB,LB))+[NB]:
            r1=min(r0+LB,T) if r0<NB else T
            m=blk(off+r0//LB-kk) if r0<NB else a_ref[:,pl.ds(c0,LB)]
            c_ref[r0:r1,:]=m-mul3(hi_ref[r0:r1,:],lo_ref[r0:r1,:],rh)
        kn=jnp.minimum(kk+1,7); n0=pl.multiple_of(kn*LB,LB)
        nh=hi_ref[pl.ds(n0,LB),:]; nl=lo_ref[pl.ds(n0,LB),:]
        dn=blk(kn*8-lax.shift_right_logical(kn*(kn-1),1))-mul3(nh,nl,jnp.concatenate([nh,nl],axis=0))
        xn=splitx(jnp.concatenate(X,axis=0))
        xs_ref[...]=xn
        ph,plo=split(c_ref[pl.ds(n0,LB),:])
        l=mul3(ph,plo,xn)
        h,lw=split(l)
        d_ref[...]=dn-mul3(h,lw,jnp.concatenate([h,lw],axis=0))
        return 0
    lax.fori_loop(0,8,body,0)
    ph,plo=split(c_ref[NB:T,:])
    q_ref[:,7*LB:]=mul3(ph,plo,xs_ref[...])

def chol(g,a):
    V=pl.BlockSpec(memory_space=pltpu.VMEM)
    return pl.pallas_call(kern, out_shape=jax.ShapeDtypeStruct((R,NB), F),
        in_specs=[V,V], out_specs=V, name="cholk",
        scratch_shapes=[pltpu.VMEM((T,NB),BF),pltpu.VMEM((T,NB),BF),pltpu.VMEM((T,LB),F),pltpu.VMEM((2*LB,LB),BF),pltpu.VMEM((LB,LB),F),pltpu.VMEM((LB,LB),F)],
        compiler_params=pltpu.CompilerParams(vmem_limit_bytes=40*1024*1024))(g,a)
NB=1024; R=160; LB=128; NG=20480
F=jnp.float32; BF=jnp.bfloat16
NN=(((1,),(0,)),((),()))
MESH=pl.DeviceIdType.MESH
def dnn(a,b): return lax.dot_general(a,b,NN,preferred_element_type=F)
def split(x):
    hi=x.astype(BF); lo=(x-hi.astype(F)).astype(BF)
    return hi,lo
ROWS=36*64; TH=ROWS//3; CH=TH//4; SC=CH//4
OFF=[j*8-j*(j-1)//2 for j in range(9)]

def comm_kern(a_ref, g_ref, b_ref, ah, al, th, tl, p_ref, r1, acc1, r2, acc2, r3, ssem, rsem):
    row=lax.axis_index("row"); col=lax.axis_index("col")
    core=lax.rem(row,2); crd=[lax.rem(col,4), lax.div(row,2), lax.div(col,4)]
    def dev(c,k): return (c[1]*2+k, c[2]*4+c[0])
    def peer(ax,o):
        c=list(crd); c[ax]=lax.rem(crd[ax]+o,4); return dev(c,core), c[ax]
    def src(ax,o): return lax.rem(crd[ax]+(4-o),4)
    partner=dev(crd,1-core)
    bar=pltpu.get_barrier_semaphore()
    pl.semaphore_signal(bar,inc=1,device_id=partner,device_id_type=MESH)
    for ax in range(3):
        for o in (1,2,3):
            pl.semaphore_signal(bar,inc=1,device_id=peer(ax,o)[0],device_id_type=MESH)
    pl.semaphore_wait(bar,10)
    sends=[]
    def rc(s,d,k,to):
        c=pltpu.make_async_remote_copy(src_ref=s,dst_ref=d,send_sem=ssem.at[k],recv_sem=rsem.at[k],device_id=to,device_id_type=MESH)
        return c
    ca=rc(a_ref,b_ref,0,partner); ca.start(); sends.append(ca)
    def put(x,r0):
        h,l=split(x)
        ah[r0:r0+R,:]=h; al[r0:r0+R,:]=l
    put(a_ref[...]*(1.0/NG),0) if False else put(a_ref[...],0)
    ca.wait_recv()
    put(b_ref[...],R)
    h64=pl.multiple_of(core*64,64)
    for i in range(8):
        th[i*LB:(i+1)*LB,:]=ah[:,i*LB:(i+1)*LB].T
        tl[i*LB:(i+1)*LB,:]=al[:,i*LB:(i+1)*LB].T
    lh=jnp.concatenate([th[pl.ds(i*LB+h64,64),:] for i in range(8)],axis=0)
    ll=jnp.concatenate([tl[pl.ds(i*LB+h64,64),:] for i in range(8)],axis=0)
    for j in range(8):
        bh=ah[:,j*LB:(j+1)*LB]; bl_=al[:,j*LB:(j+1)*LB]
        t=dnn(lh[64*j:],jnp.concatenate([bh,bl_],axis=1))
        p_ref[OFF[j]*64:OFF[j+1]*64,:]=(t[:,:LB]+t[:,LB:]+dnn(ll[64*j:],bh))*(1.0/NG)
    al8=lambda v: pl.multiple_of(v,16)
    def K(st,t,o): return 1+st*9+t*3+(o-1)
    A1=[0,1,2]; A2=[1,2,0]; A3=[2,0,1]
    c1={}
    for t in range(3):
        for o in (2,1,3):
            d,ci=peer(A1[t],o)
            c=rc(p_ref.at[pl.ds(al8(t*TH+ci*CH),CH),:], r1.at[t,o-1], K(0,t,o), d); c.start(); sends.append(c); c1[t,o]=c
    c2={}
    for t in range(3):
        for o in (1,2,3): c1[t,o].wait_recv()
        acc1[t]=p_ref[pl.ds(al8(t*TH+crd[A1[t]]*CH),CH),:]+r1[t,0]+r1[t,1]+r1[t,2]
        for o in (2,1,3):
            d,ci=peer(A2[t],o)
            c=rc(acc1.at[t,pl.ds(al8(ci*SC),SC),:], r2.at[t,o-1], K(1,t,o), d); c.start(); sends.append(c); c2[t,o]=c
    c3={}
    for t in range(3):
        for o in (1,2,3): c2[t,o].wait_recv()
        acc2[t]=acc1[t,pl.ds(al8(crd[A2[t]]*SC),SC),:]+r2[t,0]+r2[t,1]+r2[t,2]
        for o in (2,1,3):
            d,ci=peer(A3[t],o)
            c=rc(acc2.at[t], r3.at[t,o-1], K(2,t,o), d); c.start(); sends.append(c); c3[t,o]=c
    for t in range(3):
        for o in (1,2,3): c3[t,o].wait_recv()
        me=t*TH+crd[A1[t]]*CH+crd[A2[t]]*SC
        g_ref[core,pl.ds(al8(me),SC),:]=acc2[t]+r3[t,0]+r3[t,1]+r3[t,2]
        for o in (2,1,3):
            d,ci=peer(A2[t],o)
            s=g_ref.at[core,pl.ds(al8(me),SC),:]
            c=rc(s,s,K(3,t,o),d); c.start(); sends.append(c)
    for t in range(3):
        for o in (1,2,3):
            s=g_ref.at[core,pl.ds(al8(t*TH+crd[A1[t]]*CH+src(A2[t],o)*SC),SC),:]
            rc(s,s,K(3,t,o),partner).wait_recv()
        s=g_ref.at[core,pl.ds(al8(t*TH+crd[A1[t]]*CH),CH),:]
        for o in (2,1,3):
            d,ci=peer(A1[t],o)
            c=rc(s,s,K(4,t,o),d); c.start(); sends.append(c)
    for t in range(3):
        for o in (1,2,3):
            s=g_ref.at[core,pl.ds(al8(t*TH+src(A1[t],o)*CH),CH),:]
            rc(s,s,K(4,t,o),partner).wait_recv()
        s=g_ref.at[core,pl.ds(t*TH,TH),:]
        c=rc(s,s,46+t,partner); c.start(); sends.append(c)
    for t in range(3):
        s=g_ref.at[1-core,pl.ds(t*TH,TH),:]
        rc(s,s,46+t,partner).wait_recv()
    for c in sends: c.wait_send()

def gram_ar(a):
    V=pl.BlockSpec(memory_space=pltpu.VMEM)
    VM=pltpu.VMEM
    return pl.pallas_call(comm_kern, out_shape=jax.ShapeDtypeStruct((2,ROWS,LB),F),
        in_specs=[V], out_specs=V, name="gram_ar",
        scratch_shapes=[VM((R,NB),F),VM((2*R,NB),BF),VM((2*R,NB),BF),VM((NB,2*R),BF),VM((NB,2*R),BF),
            VM((ROWS,LB),F),VM((3,3,CH,LB),F),VM((3,CH,LB),F),VM((3,3,SC,LB),F),VM((3,SC,LB),F),VM((3,3,SC,LB),F),
            pltpu.SemaphoreType.DMA((49,)),pltpu.SemaphoreType.DMA((49,))],
        compiler_params=pltpu.CompilerParams(collective_id=0,has_side_effects=True,vmem_limit_bytes=40*1024*1024))(a)
def solution(mesh):
    def body(a):
        return chol(gram_ar(a), a)
    spec = P_(("row", "col"), None)
    return jax.shard_map(body, mesh=mesh, in_specs=spec, out_specs=spec, check_vma=False)
```

time: 522 us -> 78.9 us (0.15)
  other arithmetic: 266 us -> 0 us
  waiting for transfers between devices: 157 us -> 0 us
  Pallas kernels: 0 us -> 76.4 us
  matrix products: 41.5 us -> 0 us
  local copies, waits for them, and re-layouts: 33.6 us -> 1.09 us
  between operations: 18.7 us -> 0.01 us
    another operation x33 -> x0, other arithmetic: 256 us -> none  [the longest x30 173 us: reference(): factor = jnp.linalg.cholesky(margin)]
    dot_general x1 -> x0, waiting for transfers between devices: 157 us -> none  [reference(): jnp.dot(coefficients.T, coefficients, precision=lax.Precision.HIGHEST, pr...]
    pallas_call x0 -> x2, Pallas kernels: none -> 76.4 us  [the longest x1 40.4 us: chol(): pl.pallas_call(kern, out_shape=jax.ShapeDtypeStruct((R, NB), F), in_specs...]
    another operation x29 -> x0, matrix products: 34.7 us -> none  [the longest x14 23.1 us: reference(): factor = jnp.linalg.cholesky(margin)]
    another operation x33 -> x0, local copies, waits for them, and re-layouts: 25.2 us -> none
    div x2 -> x0, other arithmetic: 9.55 us -> none  [the longest x1 5.08 us: reference(): jnp.dot(coefficients.T, coefficients, precision=lax.Precision.HIGHEST, pr...]
    dot_general x1 -> x0, matrix products: 6.82 us -> none  [reference(): jnp.dot(coefficients.T, coefficients, precision=lax.Precision.HIGHEST, pr...]
    div x1 -> x0, local copies, waits for them, and re-layouts: 5.61 us -> none  [reference(): jnp.dot(coefficients.T, coefficients, precision=lax.Precision.HIGHEST, pr...]
  transfers between devices with their start and end apart: 1 -> 0, of which waited for: 1 -> 0; matrix products, arithmetic and copies ran while one was open for 0% -> 0% of each run, Pallas kernels for 0% -> 0%
where the time goes in v1:
time: 78.9 us; the launch traced here: 77.5 us
  Pallas kernels  76.4 us (97%)
  local copies, waits for them, and re-layouts  1.09 us (1%)
    pallas_call x1, Pallas kernels, chol(): pl.pallas_call(kern, out_shape=jax.ShapeDtypeStruct((R, NB), F), in_specs...  40.4 us
    pallas_call x1, Pallas kernels, gram_ar(): pl.pallas_call(comm_kern, out_shape=jax.ShapeDtypeStruct((2, ROWS, LB), F...  36 us

profile of v1, /device:TPU:0, one launch (start us, length us, event | category | flops | bytes accessed | tf_op | source)
XLA Modules:
  0.0 77.5 jit_solution(8723270401481030848)
XLA Ops:
  0.0 0.0 copy-start
  0.0 1.1 %copy-done = f32[160,1024]{1,0:T(8,128)S(1)} copy-done((f32[160,1024]{1,0:T(8,128)S(1)}, f32[160,1024]{1,0:T(8,128)}, u32[]{:S(2)}) %copy-start) | copy-done | bytes 655384
  1.1 36.0 %gram_ar.1.g_ref = f32[2,2304,128]{2,1,0:T(8,128)S(1)} custom-call(f32[160,1024]{1,0:T(8,128)S(1)} %copy-done), custom_call_target="tpu_custom_call" | custom-call | tf_op jit(solution)/shard_map/gram_ar/pallas_call | solution.py:197
  37.1 40.4 %cholk.1 = f32[160,1024]{1,0:T(8,128)} custom-call(f32[2,2304,128]{2,1,0:T(8,128)S(1)} %gram_ar.1.g_ref, f32[160,1024]{1,0:T(8,128)S(1)} %copy-done), custom_call_target="tpu_custom_call" | custom-call | tf_op jit(solution)/shard_map/cholk/pallas_call | solution.py:95
Async XLA Ops:
  0.0 1.1 %copy-start = (f32[160,1024]{1,0:T(8,128)S(1)}, f32[160,1024]{1,0:T(8,128)}, u32[]{:S(2)}) copy-start(f32[160,1024]{1,0:T(8,128)} %a_ref.3) | copy-start | bytes 1966084

commit v2 on v1

--- a/solution.py
+++ b/solution.py
@@ -6,35 +6,62 @@
 from jax.sharding import PartitionSpec as P_
 
 def bl(x, c):
-    return jnp.broadcast_to(x[:, c:c+1], (8,128))
+    return jnp.take_along_axis(x, jnp.full((8,128), c, jnp.int32), axis=1, mode='promise_in_bounds')
 def bs(x, k):
     return jnp.broadcast_to(x[k:k+1, :], (8,128))
 
-def leaf(W, nb=16):
+def leaf(W):
+    BF=jnp.bfloat16; F=jnp.float32
     sub = lax.broadcasted_iota(jnp.int32, (8,128), 0)
     lane = lax.broadcasted_iota(jnp.int32, (8,128), 1)
-    X = [jnp.where(lane == sub + 8*g, 1.0, 0.0).astype(jnp.float32) for g in range(nb)]
+    X = [jnp.where(lane == sub + 8*g, 1.0, 0.0).astype(F) for g in range(16)]
     W = list(W)
-    out = []
-    for g in range(nb):
-        C = [[bl(W[h], 8*g+k) for k in range(8)] for h in range(g, nb)]
-        fin = None
-        for k in range(8):
-            d = bs(C[0][k], k)
-            r = lax.rsqrt(d)
-            for c in C: c[k] = c[k]*r
-            for j in range(k+1, 8):
-                s = bs(C[0][k], j)
-                for c in C: c[j] = c[j] - c[k]*s
-            uW = bs(W[g], k)*r
-            uX = bs(X[g], k)*r
-            fin = uX if fin is None else jnp.where(sub == k, uX, fin)
-            for i, c in enumerate(C):
-                h = g+i
-                if h == g and k == 7: continue
-                W[h] = W[h] - c[k]*uW
-                X[h] = X[h] - c[k]*uX
-        out.append(fin)
+    out = [None]*16
+    for G in range(8):
+        g0, g1 = 2*G, 2*G+1
+        nxt = list(range(2*G+2, min(2*G+6,16)))
+        base = 16*G
+        C = {}
+        for k in range(16):
+            for h in ([g0] if k < 8 else []) + [g1] + nxt:
+                C[h, k] = bl(W[h], base+k)
+        U = {}
+        dn = None
+        for k in range(16):
+            own, i = (g0, k) if k < 8 else (g1, k-8)
+            act = ([g0] if k < 8 else []) + [g1] + nxt
+            d = bs(C[own, k], i) if dn is None else dn
+            r = 1.0/d
+            rs = lax.rsqrt(d)
+            if k < 15:
+                o2, i2 = (g0, k+1) if k+1 < 8 else (g1, k-7)
+                cc = bs(C[o2, k], i2)
+                dn = bs(C[o2, k+1], i2) - (cc*cc)*r
+            m = {h: C[h, k]*r for h in act}
+            for j in range(k+1, 16):
+                s = bs(C[g0, k], j) if j < 8 else bs(C[g1, k], j-8)
+                for h in ([g0] if j < 8 else []) + [g1] + nxt:
+                    C[h, j] = C[h, j] - m[h]*s
+            wr = bs(W[own], i)
+            xr = bs(X[own], i)
+            for h in act:
+                if h == own and i == 7: continue
+                W[h] = W[h] - m[h]*wr
+                X[h] = X[h] - m[h]*xr
+            fx = xr*rs
+            out[own] = fx if i == 0 else jnp.where(sub == i, fx, out[own])
+            if G < 5:
+                fw = wr*rs
+                U[own] = fw if i == 0 else jnp.where(sub == i, fw, U[own])
+        if G < 5:
+            u = jnp.concatenate([jnp.concatenate([U[g0], out[g0]], axis=1), jnp.concatenate([U[g1], out[g1]], axis=1)], axis=0)
+            h = u.astype(BF); l = (u - h.astype(F)).astype(BF)
+            a = jnp.concatenate([h[:, :128], h[:, :128], l[:, :128]], axis=0)
+            b = jnp.concatenate([h, l, h], axis=0)
+            upd = lax.dot_general(a, b, (((0,),(0,)),((),())), preferred_element_type=F)
+            for q in range(2*G+6, 16):
+                W[q] = W[q] - upd[8*q:8*q+8, :128]
+                X[q] = X[q] - upd[8*q:8*q+8, 128:]
     return out
 
 NB=1024; R=160; LB=128; T=NB+R
@@ -57,27 +84,26 @@
     def mul3(ph,plo,r):
         t=dnt(ph,r)
         return t[:,:LB]+t[:,LB:]+dnt(plo,r[:LB])
-    def body(kk,_):
+    def mk(rlo,K):
+      def body(kk,_):
         c0=pl.multiple_of(kk*LB,LB)
         off=kk*8-lax.shift_right_logical(kk*(kk-1),1)
         W=[d_ref[8*g:8*g+8,:] for g in range(16)]
         X=leaf(W)
         cp=pl.multiple_of(jnp.maximum(kk-1,0)*LB,LB)
         xs=xs_ref[...]
-        for r0 in list(range(0,NB,LB))+[NB]:
-            r1=min(r0+LB,T) if r0<NB else T
-            ph,plo=split(c_ref[r0:r1,:])
-            l=mul3(ph,plo,xs)
-            h,lw=split(l)
-            hi_ref[r0:r1,pl.ds(cp,LB)]=h; lo_ref[r0:r1,pl.ds(cp,LB)]=lw
-            if r0==NB: q_ref[:,pl.ds(cp,LB)]=l
-        rh=jnp.concatenate([hi_ref[pl.ds(c0,LB),:],lo_ref[pl.ds(c0,LB),:]],axis=0)
-        for r0 in list(range(0,NB,LB))+[NB]:
-            r1=min(r0+LB,T) if r0<NB else T
-            m=blk(off+r0//LB-kk) if r0<NB else a_ref[:,pl.ds(c0,LB)]
-            c_ref[r0:r1,:]=m-mul3(hi_ref[r0:r1,:],lo_ref[r0:r1,:],rh)
+        ph,plo=split(c_ref[rlo:T,:])
+        l=mul3(ph,plo,xs)
+        h,lw=split(l)
+        hi_ref[rlo:T,pl.ds(cp,LB)]=h; lo_ref[rlo:T,pl.ds(cp,LB)]=lw
+        q_ref[:,pl.ds(cp,LB)]=l[NB-rlo:]
+        rh=jnp.concatenate([hi_ref[pl.ds(c0,LB),0:K],lo_ref[pl.ds(c0,LB),0:K]],axis=0)
+        u=mul3(hi_ref[rlo:T,0:K],lo_ref[rlo:T,0:K],rh)
+        for r0 in range(rlo,NB,LB):
+            c_ref[r0:r0+LB,:]=blk(off+r0//LB-kk)-u[r0-rlo:r0-rlo+LB]
+        c_ref[NB:T,:]=a_ref[:,pl.ds(c0,LB)]-u[NB-rlo:]
         kn=jnp.minimum(kk+1,7); n0=pl.multiple_of(kn*LB,LB)
-        nh=hi_ref[pl.ds(n0,LB),:]; nl=lo_ref[pl.ds(n0,LB),:]
+        nh=hi_ref[pl.ds(n0,LB),0:K]; nl=lo_ref[pl.ds(n0,LB),0:K]
         dn=blk(kn*8-lax.shift_right_logical(kn*(kn-1),1))-mul3(nh,nl,jnp.concatenate([nh,nl],axis=0))
         xn=splitx(jnp.concatenate(X,axis=0))
         xs_ref[...]=xn
@@ -86,7 +112,9 @@
         h,lw=split(l)
         d_ref[...]=dn-mul3(h,lw,jnp.concatenate([h,lw],axis=0))
         return 0
-    lax.fori_loop(0,8,body,0)
+      return body
+    lax.fori_loop(0,4,mk(0,512),0)
+    lax.fori_loop(4,8,mk(512,1024),0)
     ph,plo=split(c_ref[NB:T,:])
     q_ref[:,7*LB:]=mul3(ph,plo,xs_ref[...])
 

time: 78.9 us -> 67.3 us (0.85)
  the two profiles are of different devices: /device:TPU:0 before, /device:TPU:1 now
where the time goes in v2:
time: 67.3 us; the launch traced here: 67.1 us
  Pallas kernels  66 us (98%)
  local copies, waits for them, and re-layouts  1.09 us (2%)
    pallas_call x1, Pallas kernels, gram_ar(): pl.pallas_call(comm_kern, out_shape=jax.ShapeDtypeStruct((2, ROWS, LB), F...  37.3 us
    pallas_call x1, Pallas kernels, chol(): pl.pallas_call(kern, out_shape=jax.ShapeDtypeStruct((R, NB), F), in_specs...  28.7 us

profile of v2, /device:TPU:1, one launch (start us, length us, event | category | flops | bytes accessed | tf_op | source)
XLA Modules:
  0.0 67.1 jit_solution(15410310338682446703)
XLA Ops:
  0.0 0.0 copy-start
  0.0 1.1 %copy-done = f32[160,1024]{1,0:T(8,128)S(1)} copy-done((f32[160,1024]{1,0:T(8,128)S(1)}, f32[160,1024]{1,0:T(8,128)}, u32[]{:S(2)}) %copy-start) | copy-done | bytes 655384
  1.1 37.3 %gram_ar.1.g_ref = f32[2,2304,128]{2,1,0:T(8,128)S(1)} custom-call(f32[160,1024]{1,0:T(8,128)S(1)} %copy-done), custom_call_target="tpu_custom_call" | custom-call | tf_op jit(solution)/shard_map/gram_ar/pallas_call | solution.py:225
  38.4 28.7 %cholk.1 = f32[160,1024]{1,0:T(8,128)} custom-call(f32[2,2304,128]{2,1,0:T(8,128)S(1)} %gram_ar.1.g_ref, f32[160,1024]{1,0:T(8,128)S(1)} %copy-done), custom_call_target="tpu_custom_call" | custom-call | tf_op jit(solution)/shard_map/cholk/pallas_call | solution.py:123
Async XLA Ops:
  0.0 1.1 %copy-start = (f32[160,1024]{1,0:T(8,128)S(1)}, f32[160,1024]{1,0:T(8,128)}, u32[]{:S(2)}) copy-start(f32[160,1024]{1,0:T(8,128)} %a_ref.3) | copy-start | bytes 1966084

commit v3 on v2

v3 whole, which is shorter than its diff:
```python
import jax
import jax.numpy as jnp
from jax import lax
from jax.experimental import pallas as pl
from jax.experimental.pallas import tpu as pltpu
from jax.sharding import PartitionSpec as P_

def bl(x, c):
    return jnp.take_along_axis(x, jnp.full((8,128), c, jnp.int32), axis=1, mode='promise_in_bounds')
def bs(x, k):
    return jnp.broadcast_to(x[k:k+1, :], (8,128))

def leaf(W):
    BF=jnp.bfloat16; F=jnp.float32
    sub = lax.broadcasted_iota(jnp.int32, (8,128), 0)
    lane = lax.broadcasted_iota(jnp.int32, (8,128), 1)
    X = [jnp.where(lane == sub + 8*g, 1.0, 0.0).astype(F) for g in range(16)]
    W = list(W)
    out = [None]*16
    for G in range(8):
        g0, g1 = 2*G, 2*G+1
        nxt = list(range(2*G+2, min(2*G+6,16)))
        base = 16*G
        C = {}
        for k in range(16):
            for h in ([g0] if k < 8 else []) + [g1] + nxt:
                C[h, k] = bl(W[h], base+k)
        U = {}
        dn = None
        for k in range(16):
            own, i = (g0, k) if k < 8 else (g1, k-8)
            act = ([g0] if k < 8 else []) + [g1] + nxt
            d = bs(C[own, k], i) if dn is None else dn
            r = 1.0/d
            rs = lax.rsqrt(d)
            if k < 15:
                o2, i2 = (g0, k+1) if k+1 < 8 else (g1, k-7)
                cc = bs(C[o2, k], i2)
                dn = bs(C[o2, k+1], i2) - (cc*cc)*r
            m = {h: C[h, k]*r for h in act}
            for j in range(k+1, 16):
                s = bs(C[g0, k], j) if j < 8 else bs(C[g1, k], j-8)
                for h in ([g0] if j < 8 else []) + [g1] + nxt:
                    C[h, j] = C[h, j] - m[h]*s
            wr = bs(W[own], i)
            xr = bs(X[own], i)
            for h in act:
                if h == own and i == 7: continue
                W[h] = W[h] - m[h]*wr
                X[h] = X[h] - m[h]*xr
            fx = xr*rs
            out[own] = fx if i == 0 else jnp.where(sub == i, fx, out[own])
            if G < 5:
                fw = wr*rs
                U[own] = fw if i == 0 else jnp.where(sub == i, fw, U[own])
        if G < 5:
            u = jnp.concatenate([jnp.concatenate([U[g0], out[g0]], axis=1), jnp.concatenate([U[g1], out[g1]], axis=1)], axis=0)
            h = u.astype(BF); l = (u - h.astype(F)).astype(BF)
            a = jnp.concatenate([h[:, :128], h[:, :128], l[:, :128]], axis=0)
            b = jnp.concatenate([h, l, h], axis=0)
            upd = lax.dot_general(a, b, (((0,),(0,)),((),())), preferred_element_type=F)
            for q in range(2*G+6, 16):
                W[q] = W[q] - upd[8*q:8*q+8, :128]
                X[q] = X[q] - upd[8*q:8*q+8, 128:]
    return out


NB=1024; R=160; LB=128; T=NB+R; NG=20480
F=jnp.float32; BF=jnp.bfloat16
NT=(((1,),(1,)),((),())); NN=(((1,),(0,)),((),()))
MESH=pl.DeviceIdType.MESH
def dnt(a,b): return lax.dot_general(a,b,NT,preferred_element_type=F)
def dnn(a,b): return lax.dot_general(a,b,NN,preferred_element_type=F)
def split(x):
    hi=x.astype(BF); lo=(x-hi.astype(F)).astype(BF)
    return hi,lo
ROWS=36*64; PH=ROWS//3; TH=PH//3; CH=TH//4; SC=CH//4
OFF=[j*8-j*(j-1)//2 for j in range(9)]

def kernel(a_ref, q_ref, g_ref, b_ref, ah, al, th, tl, p_ref, r1, acc1, r2, acc2, r3,
           hi_ref, lo_ref, c_ref, xs_ref, d_ref, ssem, rsem):
    row=lax.axis_index("row"); col=lax.axis_index("col")
    core=lax.rem(row,2); crd=[lax.rem(col,4), lax.div(row,2), lax.div(col,4)]
    def dev(c,k): return (c[1]*2+k, c[2]*4+c[0])
    def peer(ax,o):
        c=list(crd); c[ax]=lax.rem(crd[ax]+o,4); return dev(c,core), c[ax]
    def src(ax,o): return lax.rem(crd[ax]+(4-o),4)
    partner=dev(crd,1-core)
    bar=pltpu.get_barrier_semaphore()
    pl.semaphore_signal(bar,inc=1,device_id=partner,device_id_type=MESH)
    for ax in range(3):
        for o in (1,2,3):
            pl.semaphore_signal(bar,inc=1,device_id=peer(ax,o)[0],device_id_type=MESH)
    sends=[]
    def rc(s,d,k,to):
        return pltpu.make_async_remote_copy(src_ref=s,dst_ref=d,send_sem=ssem.at[k],recv_sem=rsem.at[k],device_id=to,device_id_type=MESH)
    def go(s,d,k,to):
        c=rc(s,d,k,to); c.start(); sends.append(c); return c
    def prep(x,n):
        h,l=split(x)
        ah[n]=h; al[n]=l
        for i in range(8):
            th[n,i*LB:(i+1)*LB,:]=h[:,i*LB:(i+1)*LB].T
            tl[n,i*LB:(i+1)*LB,:]=l[:,i*LB:(i+1)*LB].T
    h64=pl.multiple_of(core*64,64)
    def gram(n,js):
        lh=jnp.concatenate([th[n,pl.ds(i*LB+h64,64),:] for i in range(js[0],8)],axis=0)
        ll=jnp.concatenate([tl[n,pl.ds(i*LB+h64,64),:] for i in range(js[0],8)],axis=0)
        for j in js:
            bh=ah[n,:,j*LB:(j+1)*LB]; bl_=al[n,:,j*LB:(j+1)*LB]
            z=64*(j-js[0])
            t=dnn(lh[z:],jnp.concatenate([bh,bl_],axis=1))
            u=t[:,:LB]+t[:,LB:]+dnn(ll[z:],bh)
            s=slice(OFF[j]*64,OFF[j+1]*64)
            if n==0: p_ref[s,:]=u
            else: p_ref[s,:]=(p_ref[s,:]+u)*(1.0/NG)
    pl.semaphore_wait(bar,10)
    ca=go(a_ref,b_ref,0,partner)
    prep(a_ref[...],0)
    gram(0,list(range(8)))
    ca.wait_recv()
    prep(b_ref[...],1)
    al8=lambda v: pl.multiple_of(v,16)
    def K(f,st,t,o): return 1+(f*5+st)*9+t*3+(o-1)
    A1=[0,1,2]; A2=[1,2,0]; A3=[2,0,1]
    OS=(2,1,3); C={}
    def st1(f):
        for t in range(3):
            for o in OS:
                d,ci=peer(A1[t],o)
                C[f,1,t,o]=go(p_ref.at[pl.ds(al8(f*PH+t*TH+ci*CH),CH),:], r1.at[f,t,o-1], K(f,0,t,o), d)
    def st2(f):
        for t in range(3):
            for o in OS: C[f,1,t,o].wait_recv()
            acc1[f,t]=p_ref[pl.ds(al8(f*PH+t*TH+crd[A1[t]]*CH),CH),:]+r1[f,t,0]+r1[f,t,1]+r1[f,t,2]
            for o in OS:
                d,ci=peer(A2[t],o)
                C[f,2,t,o]=go(acc1.at[f,t,pl.ds(al8(ci*SC),SC),:], r2.at[f,t,o-1], K(f,1,t,o), d)
    def st3(f):
        for t in range(3):
            for o in OS: C[f,2,t,o].wait_recv()
            acc2[f,t]=acc1[f,t,pl.ds(al8(crd[A2[t]]*SC),SC),:]+r2[f,t,0]+r2[f,t,1]+r2[f,t,2]
            for o in OS:
                d,ci=peer(A3[t],o)
                C[f,3,t,o]=go(acc2.at[f,t], r3.at[f,t,o-1], K(f,2,t,o), d)
    def mine(f,t): return f*PH+t*TH+crd[A1[t]]*CH
    def st4(f):
        for t in range(3):
            for o in OS: C[f,3,t,o].wait_recv()
            me=al8(mine(f,t)+crd[A2[t]]*SC)
            g_ref[core,pl.ds(me,SC),:]=acc2[f,t]+r3[f,t,0]+r3[f,t,1]+r3[f,t,2]
            s=g_ref.at[core,pl.ds(me,SC),:]
            for o in OS: go(s,s,K(f,3,t,o),peer(A2[t],o)[0])
    def st5(f):
        for t in range(3):
            for o in OS:
                s=g_ref.at[core,pl.ds(al8(mine(f,t)+src(A2[t],o)*SC),SC),:]
                rc(s,s,K(f,3,t,o),partner).wait_recv()
            s=g_ref.at[core,pl.ds(al8(mine(f,t)),CH),:]
            for o in OS: go(s,s,K(f,4,t,o),peer(A1[t],o)[0])
    def c6(f,t,k):
        s=g_ref.at[k,pl.ds(f*PH+t*TH,TH),:]
        return rc(s,s,136+f*3+t,partner)
    def st6(f,keep=True):
        for t in range(3):
            for o in OS:
                s=g_ref.at[core,pl.ds(al8(f*PH+t*TH+src(A1[t],o)*CH),CH),:]
                rc(s,s,K(f,4,t,o),partner).wait_recv()
            c6(f,t,core).start()
    def fin(f):
        for t in range(3): c6(f,t,1-core).wait_recv()
    gram(1,[0,1])
    st1(0)
    gram(1,[2,3,4,5,6,7])
    st1(1); st2(0); st1(2)
    def comm_rest():
        st3(0); st2(1)
        st4(0); st3(1); st2(2)
        st5(0); st4(1); st3(2)
        st6(0); st5(1); st4(2)
        fin(0); st6(1); st5(2)
    def hook(kk):
        @pl.when(kk==1)
        def _():
            fin(1); st6(2)
        @pl.when(kk==3)
        def _():
            fin(2)
    hi_ref[...]=jnp.zeros_like(hi_ref); lo_ref[...]=jnp.zeros_like(lo_ref)
    c_ref[...]=jnp.zeros_like(c_ref); xs_ref[...]=jnp.zeros_like(xs_ref)
    def blk(p):
        return jnp.concatenate([g_ref[0,pl.ds(p*64,64),:],g_ref[1,pl.ds(p*64,64),:]],axis=0)
    def splitx(x):
        xh,xl=split(x)
        return jnp.concatenate([xh,xl],axis=0)
    def mul3(ph,plo,r):
        t=dnt(ph,r)
        return t[:,:LB]+t[:,LB:]+dnt(plo,r[:LB])
    def mk(rlo,K):
      def body(kk,_):
        if rlo==0: hook(kk)
        c0=pl.multiple_of(kk*LB,LB)
        off=kk*8-lax.shift_right_logical(kk*(kk-1),1)
        W=[d_ref[8*g:8*g+8,:] for g in range(16)]
        X=leaf(W)
        cp=pl.multiple_of(jnp.maximum(kk-1,0)*LB,LB)
        xs=xs_ref[...]
        ph,plo=split(c_ref[rlo:T,:])
        l=mul3(ph,plo,xs)
        h,lw=split(l)
        hi_ref[rlo:T,pl.ds(cp,LB)]=h; lo_ref[rlo:T,pl.ds(cp,LB)]=lw
        q_ref[:,pl.ds(cp,LB)]=l[NB-rlo:]
        rh=jnp.concatenate([hi_ref[pl.ds(c0,LB),0:K],lo_ref[pl.ds(c0,LB),0:K]],axis=0)
        u=mul3(hi_ref[rlo:T,0:K],lo_ref[rlo:T,0:K],rh)
        for r0 in range(rlo,NB,LB):
            c_ref[r0:r0+LB,:]=blk(off+r0//LB-kk)-u[r0-rlo:r0-rlo+LB]
        c_ref[NB:T,:]=a_ref[:,pl.ds(c0,LB)]-u[NB-rlo:]
        kn=jnp.minimum(kk+1,7); n0=pl.multiple_of(kn*LB,LB)
        nh=hi_ref[pl.ds(n0,LB),0:K]; nl=lo_ref[pl.ds(n0,LB),0:K]
        dn=blk(kn*8-lax.shift_right_logical(kn*(kn-1),1))-mul3(nh,nl,jnp.concatenate([nh,nl],axis=0))
        xn=splitx(jnp.concatenate(X,axis=0))
        xs_ref[...]=xn
        ph,plo=split(c_ref[pl.ds(n0,LB),:])
        l=mul3(ph,plo,xn)
        h,lw=split(l)
        d_ref[...]=dn-mul3(h,lw,jnp.concatenate([h,lw],axis=0))
        return 0
      return body
    comm_rest()
    d_ref[...]=blk(0)
    lax.fori_loop(0,4,mk(0,512),0)
    lax.fori_loop(4,8,mk(512,1024),0)
    ph,plo=split(c_ref[NB:T,:])
    q_ref[:,7*LB:]=mul3(ph,plo,xs_ref[...])

    for c in sends: c.wait_send()
    for f in range(3):
        for t in range(3): c6(f,t,core).wait_send()

def solution(mesh):
    VM=pltpu.VMEM
    V=pl.BlockSpec(memory_space=VM)
    def body(a):
        return pl.pallas_call(kernel, out_shape=jax.ShapeDtypeStruct((R,NB),F),
            in_specs=[V], out_specs=V, name="ortho",
            scratch_shapes=[VM((2,ROWS,LB),F),VM((R,NB),F),VM((2,R,NB),BF),VM((2,R,NB),BF),VM((2,NB,R),BF),VM((2,NB,R),BF),
                VM((ROWS,LB),F),VM((3,3,3,CH,LB),F),VM((3,3,CH,LB),F),VM((3,3,3,SC,LB),F),VM((3,3,SC,LB),F),VM((3,3,3,SC,LB),F),
                VM((T,NB),BF),VM((T,NB),BF),VM((T,LB),F),VM((2*LB,LB),BF),VM((LB,LB),F),
                pltpu.SemaphoreType.DMA((145,)),pltpu.SemaphoreType.DMA((145,))],
            compiler_params=pltpu.CompilerParams(collective_id=0,has_side_effects=True,vmem_limit_bytes=48*1024*1024))(a)
    spec = P_(("row", "col"), None)
    return jax.shard_map(body, mesh=mesh, in_specs=spec, out_specs=spec, check_vma=False)
```

time: 67.3 us -> 65.2 us (0.969)
  the two profiles are of different devices: /device:TPU:1 before, /device:TPU:0 now
where the time goes in v3:
time: 65.2 us; the launch traced here: 65 us
  Pallas kernels  63.1 us (97%)
  local copies, waits for them, and re-layouts  1.93 us (3%)
    pallas_call x1, Pallas kernels, body(): pl.pallas_call(kernel, out_shape=jax.ShapeDtypeStruct((R, NB), F), in_spe...  63.1 us
    unnamed x3, local copies, waits for them, and re-layouts  1.93 us

profile of v3, /device:TPU:0, one launch (start us, length us, event | category | flops | bytes accessed | tf_op | source)
XLA Modules:
  0.0 65.0 jit_solution(8344458165525509130)
XLA Ops:
  0.0 0.0 copy-start
  0.0 1.1 %copy-done = f32[160,1024]{1,0:T(8,128)S(1)} copy-done((f32[160,1024]{1,0:T(8,128)S(1)}, f32[160,1024]{1,0:T(8,128)}, u32[]{:S(2)}) %copy-start) | copy-done | bytes 655384
  1.1 63.1 %ortho.1 = f32[160,1024]{1,0:T(8,128)S(1)} custom-call(f32[160,1024]{1,0:T(8,128)S(1)} %copy-done), custom_call_target="tpu_custom_call" | custom-call | tf_op jit(solution)/shard_map/ortho/pallas_call | solution.py:244
  64.2 0.8 %copy.3 = f32[160,1024]{1,0:T(8,128)} copy(f32[160,1024]{1,0:T(8,128)S(1)} %ortho.1) | data formatting | bytes 1310720
Async XLA Ops:
  0.0 1.1 %copy-start = (f32[160,1024]{1,0:T(8,128)S(1)}, f32[160,1024]{1,0:T(8,128)}, u32[]{:S(2)}) copy-start(f32[160,1024]{1,0:T(8,128)} %a_ref.1) | copy-start | bytes 1966084

commit v4 on v3

--- a/solution.py
+++ b/solution.py
@@ -10,26 +10,31 @@
 def bs(x, k):
     return jnp.broadcast_to(x[k:k+1, :], (8,128))
 
-def leaf(W):
+def leaf(W, near=4, full=2):
     BF=jnp.bfloat16; F=jnp.float32
     sub = lax.broadcasted_iota(jnp.int32, (8,128), 0)
     lane = lax.broadcasted_iota(jnp.int32, (8,128), 1)
-    X = [jnp.where(lane == sub + 8*g, 1.0, 0.0).astype(F) for g in range(16)]
     W = list(W)
     out = [None]*16
+    rv = jnp.zeros((8,128), F)
     for G in range(8):
         g0, g1 = 2*G, 2*G+1
-        nxt = list(range(2*G+2, min(2*G+6,16)))
+        nf = list(range(2*G+2, min(2*G+2+full,16)))
+        nh = list(range(2*G+2+full, min(2*G+2+near,16)))
         base = 16*G
+        far = 2*G+2+near < 16
         C = {}
         for k in range(16):
-            for h in ([g0] if k < 8 else []) + [g1] + nxt:
+            for h in ([g0] if k < 8 else []) + [g1] + nf + (nh if k < 8 else []):
                 C[h, k] = bl(W[h], base+k)
         U = {}
         dn = None
         for k in range(16):
+            if k == 8:
+                for h in nh:
+                    for kk in range(8, 16): C[h, kk] = bl(W[h], base+kk)
             own, i = (g0, k) if k < 8 else (g1, k-8)
-            act = ([g0] if k < 8 else []) + [g1] + nxt
+            act = ([g0] if k < 8 else []) + [g1] + nf + nh
             d = bs(C[own, k], i) if dn is None else dn
             r = 1.0/d
             rs = lax.rsqrt(d)
@@ -40,30 +45,35 @@
             m = {h: C[h, k]*r for h in act}
             for j in range(k+1, 16):
                 s = bs(C[g0, k], j) if j < 8 else bs(C[g1, k], j-8)
-                for h in ([g0] if j < 8 else []) + [g1] + nxt:
+                for h in ([g0] if j < 8 else []) + [g1] + nf + (nh if (j < 8 or k >= 8) else []):
                     C[h, j] = C[h, j] - m[h]*s
             wr = bs(W[own], i)
-            xr = bs(X[own], i)
+            hot = lane == base+k
+            wr2 = jnp.where(hot, wr+wr, wr)
             for h in act:
                 if h == own and i == 7: continue
-                W[h] = W[h] - m[h]*wr
-                X[h] = X[h] - m[h]*xr
-            fx = xr*rs
+                W[h] = W[h] - m[h]*wr2
+            fx = wr*rs
             out[own] = fx if i == 0 else jnp.where(sub == i, fx, out[own])
-            if G < 5:
-                fw = wr*rs
-                U[own] = fw if i == 0 else jnp.where(sub == i, fw, U[own])
-        if G < 5:
-            u = jnp.concatenate([jnp.concatenate([U[g0], out[g0]], axis=1), jnp.concatenate([U[g1], out[g1]], axis=1)], axis=0)
-            h = u.astype(BF); l = (u - h.astype(F)).astype(BF)
-            a = jnp.concatenate([h[:, :128], h[:, :128], l[:, :128]], axis=0)
+            rv = jnp.where(hot, r, rv)
+        if far:
+            u = jnp.concatenate([out[g0], out[g1]], axis=0)
+            cl = lax.broadcasted_iota(jnp.int32, (16,128), 1)
+            rw = lax.broadcasted_iota(jnp.int32, (16,128), 0)
+            ub = jnp.where((cl <= base+rw) | (cl >= base+16), u, 0.0)
+            h = ub.astype(BF); l = (ub - h.astype(F)).astype(BF)
+            ur = jnp.where(cl >= base+16, u, 0.0)
+            hr = ur.astype(BF); lr = (ur - hr.astype(F)).astype(BF)
+            a = jnp.concatenate([hr, hr, lr], axis=0)
             b = jnp.concatenate([h, l, h], axis=0)
             upd = lax.dot_general(a, b, (((0,),(0,)),((),())), preferred_element_type=F)
-            for q in range(2*G+6, 16):
-                W[q] = W[q] - upd[8*q:8*q+8, :128]
-                X[q] = X[q] - upd[8*q:8*q+8, 128:]
-    return out
-
+            keep = (lane < base) | (lane >= base+16)
+            for q in range(2*G+2+near, 16):
+                W[q] = jnp.where(keep, W[q], 0.0) - upd[8*q:8*q+8, :]
+    res = []
+    for g in range(16):
+        res.append(jnp.where(lane <= sub + 8*g, out[g]*rv, 0.0))
+    return res
 
 NB=1024; R=160; LB=128; T=NB+R; NG=20480
 F=jnp.float32; BF=jnp.bfloat16
@@ -77,8 +87,8 @@
 ROWS=36*64; PH=ROWS//3; TH=PH//3; CH=TH//4; SC=CH//4
 OFF=[j*8-j*(j-1)//2 for j in range(9)]
 
-def kernel(a_ref, q_ref, g_ref, b_ref, ah, al, th, tl, p_ref, r1, acc1, r2, acc2, r3,
-           hi_ref, lo_ref, c_ref, xs_ref, d_ref, ssem, rsem):
+def kernel(x_ref, q_ref, a_ref, g_ref, b_ref, ah, al, th, tl, p_ref, r1, acc1, r2, acc2, r3,
+           hi_ref, lo_ref, c_ref, xs_ref, d_ref, ssem, rsem, lsem):
     row=lax.axis_index("row"); col=lax.axis_index("col")
     core=lax.rem(row,2); crd=[lax.rem(col,4), lax.div(row,2), lax.div(col,4)]
     def dev(c,k): return (c[1]*2+k, c[2]*4+c[0])
@@ -114,13 +124,17 @@
             s=slice(OFF[j]*64,OFF[j+1]*64)
             if n==0: p_ref[s,:]=u
             else: p_ref[s,:]=(p_ref[s,:]+u)*(1.0/NG)
+    ld=pltpu.make_async_copy(x_ref,a_ref,lsem); ld.start()
+    hi_ref[...]=jnp.zeros_like(hi_ref); lo_ref[...]=jnp.zeros_like(lo_ref)
+    c_ref[...]=jnp.zeros_like(c_ref); xs_ref[...]=jnp.zeros_like(xs_ref)
+    ld.wait()
+    prep(a_ref[...],0)
     pl.semaphore_wait(bar,10)
     ca=go(a_ref,b_ref,0,partner)
-    prep(a_ref[...],0)
     gram(0,list(range(8)))
     ca.wait_recv()
     prep(b_ref[...],1)
-    al8=lambda v: pl.multiple_of(v,16)
+    al8=lambda v: pl.multiple_of(v,8)
     def K(f,st,t,o): return 1+(f*5+st)*9+t*3+(o-1)
     A1=[0,1,2]; A2=[1,2,0]; A3=[2,0,1]
     OS=(2,1,3); C={}
@@ -157,7 +171,7 @@
                 s=g_ref.at[core,pl.ds(al8(mine(f,t)+src(A2[t],o)*SC),SC),:]
                 rc(s,s,K(f,3,t,o),partner).wait_recv()
             s=g_ref.at[core,pl.ds(al8(mine(f,t)),CH),:]
-            for o in OS: go(s,s,K(f,4,t,o),peer(A1[t],o)[0])
+            for o in OS: rc(s,s,K(f,4,t,o),peer(A1[t],o)[0]).start()
     def c6(f,t,k):
         s=g_ref.at[k,pl.ds(f*PH+t*TH,TH),:]
         return rc(s,s,136+f*3+t,partner)
@@ -186,8 +200,6 @@
         @pl.when(kk==3)
         def _():
             fin(2)
-    hi_ref[...]=jnp.zeros_like(hi_ref); lo_ref[...]=jnp.zeros_like(lo_ref)
-    c_ref[...]=jnp.zeros_like(c_ref); xs_ref[...]=jnp.zeros_like(xs_ref)
     def blk(p):
         return jnp.concatenate([g_ref[0,pl.ds(p*64,64),:],g_ref[1,pl.ds(p*64,64),:]],axis=0)
     def splitx(x):
@@ -198,7 +210,7 @@
         return t[:,:LB]+t[:,LB:]+dnt(plo,r[:LB])
     def mk(rlo,K):
       def body(kk,_):
-        if rlo==0: hook(kk)
+        if rlo<512: hook(kk)
         c0=pl.multiple_of(kk*LB,LB)
         off=kk*8-lax.shift_right_logical(kk*(kk-1),1)
         W=[d_ref[8*g:8*g+8,:] for g in range(16)]
@@ -228,25 +240,30 @@
       return body
     comm_rest()
     d_ref[...]=blk(0)
-    lax.fori_loop(0,4,mk(0,512),0)
-    lax.fori_loop(4,8,mk(512,1024),0)
+    lax.fori_loop(0,2,mk(0,256),0)
+    lax.fori_loop(2,4,mk(256,512),0)
+    lax.fori_loop(4,6,mk(512,768),0)
+    lax.fori_loop(6,8,mk(768,1024),0)
     ph,plo=split(c_ref[NB:T,:])
     q_ref[:,7*LB:]=mul3(ph,plo,xs_ref[...])
 
     for c in sends: c.wait_send()
     for f in range(3):
-        for t in range(3): c6(f,t,core).wait_send()
+        for t in range(3):
+            c6(f,t,core).wait_send()
+            s=g_ref.at[core,pl.ds(al8(mine(f,t)),CH),:]
+            for o in OS: rc(s,s,K(f,4,t,o),partner).wait_send()
 
 def solution(mesh):
     VM=pltpu.VMEM
     V=pl.BlockSpec(memory_space=VM)
     def body(a):
         return pl.pallas_call(kernel, out_shape=jax.ShapeDtypeStruct((R,NB),F),
-            in_specs=[V], out_specs=V, name="ortho",
-            scratch_shapes=[VM((2,ROWS,LB),F),VM((R,NB),F),VM((2,R,NB),BF),VM((2,R,NB),BF),VM((2,NB,R),BF),VM((2,NB,R),BF),
+            in_specs=[pl.BlockSpec(memory_space=pltpu.HBM)], out_specs=V, name="ortho",
+            scratch_shapes=[VM((R,NB),F),VM((2,ROWS,LB),F),VM((R,NB),F),VM((2,R,NB),BF),VM((2,R,NB),BF),VM((2,NB,R),BF),VM((2,NB,R),BF),
                 VM((ROWS,LB),F),VM((3,3,3,CH,LB),F),VM((3,3,CH,LB),F),VM((3,3,3,SC,LB),F),VM((3,3,SC,LB),F),VM((3,3,3,SC,LB),F),
                 VM((T,NB),BF),VM((T,NB),BF),VM((T,LB),F),VM((2*LB,LB),BF),VM((LB,LB),F),
-                pltpu.SemaphoreType.DMA((145,)),pltpu.SemaphoreType.DMA((145,))],
+                pltpu.SemaphoreType.DMA((145,)),pltpu.SemaphoreType.DMA((145,)),pltpu.SemaphoreType.DMA],
             compiler_params=pltpu.CompilerParams(collective_id=0,has_side_effects=True,vmem_limit_bytes=48*1024*1024))(a)
     spec = P_(("row", "col"), None)
     return jax.shard_map(body, mesh=mesh, in_specs=spec, out_specs=spec, check_vma=False)

time: 65.2 us -> 63 us (0.966)
  Pallas kernels: 63.1 us -> 60.9 us
    pallas_call x1, Pallas kernels: 63.1 us -> 60.9 us  [body(): pl.pallas_call(kernel, out_shape=jax.ShapeDtypeStruct((R, NB), F), in_spe...]
where the time goes in v4:
time: 63 us; the launch traced here: 62.8 us
  Pallas kernels  60.9 us (97%)
  local copies, waits for them, and re-layouts  1.93 us (3%)
    pallas_call x1, Pallas kernels, body(): pl.pallas_call(kernel, out_shape=jax.ShapeDtypeStruct((R, NB), F), in_spe...  60.9 us
    unnamed x3, local copies, waits for them, and re-layouts  1.93 us

profile of v4, /device:TPU:0, one launch (start us, length us, event | category | flops | bytes accessed | tf_op | source)
XLA Modules:
  0.0 62.8 jit_solution(406933070312127971)
XLA Ops:
  0.0 0.0 copy-start
  0.0 1.1 %copy-done = f32[160,1024]{1,0:T(8,128)S(1)} copy-done((f32[160,1024]{1,0:T(8,128)S(1)}, f32[160,1024]{1,0:T(8,128)}, u32[]{:S(2)}) %copy-start) | copy-done | bytes 655384
  1.1 60.9 %ortho.1 = f32[160,1024]{1,0:T(8,128)S(1)} custom-call(f32[160,1024]{1,0:T(8,128)S(1)} %copy-done), custom_call_target="tpu_custom_call" | custom-call | tf_op jit(solution)/shard_map/ortho/pallas_call | solution.py:261
  62.0 0.8 %copy.3 = f32[160,1024]{1,0:T(8,128)} copy(f32[160,1024]{1,0:T(8,128)S(1)} %ortho.1) | data formatting | bytes 1310720
Async XLA Ops:
  0.0 1.1 %copy-start = (f32[160,1024]{1,0:T(8,128)S(1)}, f32[160,1024]{1,0:T(8,128)}, u32[]{:S(2)}) copy-start(f32[160,1024]{1,0:T(8,128)} %x_ref.1) | copy-start | bytes 1966084

commit v5 on v4

--- a/solution.py
+++ b/solution.py
@@ -192,11 +192,14 @@
         st4(0); st3(1); st2(2)
         st5(0); st4(1); st3(2)
         st6(0); st5(1); st4(2)
-        fin(0); st6(1); st5(2)
+        fin(0)
     def hook(kk):
         @pl.when(kk==1)
         def _():
-            fin(1); st6(2)
+            st6(1); st5(2); fin(1)
+        @pl.when(kk==2)
+        def _():
+            st6(2)
         @pl.when(kk==3)
         def _():
             fin(2)

time: 63 us -> 61.3 us (0.973); the launches traced: 62.8 us -> 60.1 us
  Pallas kernels: 60.9 us -> 58.2 us
    pallas_call x1, Pallas kernels: 60.9 us -> 58.2 us  [body(): pl.pallas_call(kernel, out_shape=jax.ShapeDtypeStruct((R, NB), F), in_spe...]
where the time goes in v5:
time: 61.3 us; the launch traced here: 60.1 us
  Pallas kernels  58.2 us (95%)
  local copies, waits for them, and re-layouts  1.93 us (3%)
    pallas_call x1, Pallas kernels, body(): pl.pallas_call(kernel, out_shape=jax.ShapeDtypeStruct((R, NB), F), in_spe...  58.2 us
    unnamed x3, local copies, waits for them, and re-layouts  1.93 us

profile of v5, /device:TPU:0, one launch (start us, length us, event | category | flops | bytes accessed | tf_op | source)
XLA Modules:
  0.0 60.1 jit_solution(14786712371247480948)
XLA Ops:
  0.0 0.0 copy-start
  0.0 1.1 %copy-done = f32[160,1024]{1,0:T(8,128)S(1)} copy-done((f32[160,1024]{1,0:T(8,128)S(1)}, f32[160,1024]{1,0:T(8,128)}, u32[]{:S(2)}) %copy-start) | copy-done | bytes 655384
  1.1 58.2 %ortho.1 = f32[160,1024]{1,0:T(8,128)S(1)} custom-call(f32[160,1024]{1,0:T(8,128)S(1)} %copy-done), custom_call_target="tpu_custom_call" | custom-call | tf_op jit(solution)/shard_map/ortho/pallas_call | solution.py:264
  59.3 0.8 %copy.3 = f32[160,1024]{1,0:T(8,128)} copy(f32[160,1024]{1,0:T(8,128)S(1)} %ortho.1) | data formatting | bytes 1310720
Async XLA Ops:
  0.0 1.1 %copy-start = (f32[160,1024]{1,0:T(8,128)S(1)}, f32[160,1024]{1,0:T(8,128)}, u32[]{:S(2)}) copy-start(f32[160,1024]{1,0:T(8,128)} %x_ref.1) | copy-start | bytes 1966084
